TPU v7x, 128 devices: a 2x2x16 block of a 8x8x16 slice. The times are simulated.
128 devices in a mesh: grp: 4 (over y, x), gx: 32 (over z, core).
Axes of the slice: x: 2, y: 2, z: 16, core: 2. Of those that a mesh axis runs over, the one named last changes fastest.
The devices are a block of a 8x8x16 slice.
Arguments:
- remaining_states: bfloat16 [512, 16384], P(('grp', 'gx')), parts along dimension 0, may hold values from -6 to 6
- scaling_factor_vector: bfloat16 [16384], replicated, may hold values from 0.25 to 1.75
- probe_projection_matrix: bfloat16 [16384, 8192], P(None, 'gx'), may hold values from -1 to 1
- memory_projection_matrix: bfloat16 [16384, 1024], P('gx'), may hold values from -0.046875 to 0.046875
- final_projection_matrix: bfloat16 [8192, 16384], P('gx'), may hold values from -0.0625 to 0.0625
- memorized_address_tensor: bfloat16 [4096, 128, 512], P(('grp', 'gx')), parts along dimension 0, may hold values from -8 to 8
- memorized_content_tensor: bfloat16 [4096, 128, 512], P(('grp', 'gx')), parts along dimension 0, may hold values from -6 to 6
- retained_sequence_ids: int32 [512], P('grp'), parts along dimension 0, may hold values from 0 to 1023, as said below
- occupied_positions: int32 [4096], P(('grp', 'gx')), parts along dimension 0, may hold values from 1 to 128
Outputs:
- result: bfloat16 [512, 16384], P(('grp', 'gx')), parts along dimension 0
There are 4 independent parts, one for each index of `grp`. A program takes and returns all parts, laid end to end along the dimension named above; an argument that names none is the same for every part. Nothing has to cross between parts.
Inputs may be any that keep to these rules, and one draw needn't show every extreme that they name: Distinct batch rows; row r of remaining_states belongs to batch row retained_sequence_ids[r].
All inputs are finite; a program needn't handle non-finite values.
Results may differ from a plain program's by a relative error of at most 0.014.
Values may be sent and summed in bfloat16 or wider, within the bound.
A program may use at most 192 MiB of HBM per device.

v0:
```python
import jax
import jax.numpy as jnp
from jax import lax
from jax.sharding import Mesh
from jax.sharding import PartitionSpec as P

HEADS = 64
KV = 4
DH = 128
CACHE = 128
GX = ("gx_0", "gx_1")
GRP_GX = ("grp", "gx_0", "gx_1")


epsilon = 1e-05


def sum_in_order(pieces, axes, sequence):
    lengths = [lax.axis_size(a) for a in axes]
    pieces = pieces.reshape(*lengths, *pieces.shape[1:])
    pieces = pieces.transpose(*sequence, *range(len(axes), pieces.ndim))
    pieces = pieces.reshape(-1, *pieces.shape[len(axes) :])
    for k in sequence:
        pieces = lax.psum_scatter(pieces, axes[k], scatter_dimension=0, tiled=True)
    return pieces[0]


def split_up(array, dim, length):
    before, after = (array.shape[:dim], array.shape[dim + 1 :])
    return jnp.moveaxis(array.reshape(*before, length, -1, *after), dim, 0)


def sum_by_axis(array, axes, sequence, dim):
    length = lax.axis_size(axes)
    return sum_in_order(split_up(array, dim, length), axes, sequence)


def normalize(remaining_states, scaling_factor_vector):
    values = remaining_states.astype(jnp.float32)
    inverse = lax.rsqrt(jnp.mean(values * values, axis=1, keepdims=True) + epsilon)
    return (values * inverse * scaling_factor_vector.astype(jnp.float32)).astype(jnp.bfloat16)


def attend_slots(probe_vectors, new_kv, keys, values, slot_lengths):
    slots = probe_vectors.shape[0]
    query_heads = probe_vectors.reshape(slots, KV, HEADS // KV, DH)
    key_heads = keys.reshape(slots, CACHE, KV, DH)
    value_heads = values.reshape(slots, CACHE, KV, DH)
    inverse = 1.0 / jnp.sqrt(jnp.float32(DH))
    scores = (
        jnp.einsum("skgd,sjkd->skgj", query_heads, key_heads, preferred_element_type=jnp.float32)
        * inverse
    )
    visible = (jnp.arange(CACHE, dtype=jnp.int32)[None, :] < slot_lengths[:, None])[
        :, None, None, :
    ]
    scores = jnp.where(visible, scores, jnp.float32(-1e30))
    new_keys = new_kv[:, : KV * DH].astype(jnp.float32).reshape(slots, KV, 1, DH)
    new_values = new_kv[:, KV * DH :].astype(jnp.float32).reshape(slots, KV, 1, DH)
    own_score = jnp.sum(query_heads.astype(jnp.float32) * new_keys, axis=-1) * inverse
    highest = jnp.maximum(jnp.max(scores, axis=-1), own_score)
    expo_cache = jnp.where(visible, jnp.exp(scores - highest[..., None]), jnp.float32(0.0))
    expo_new = jnp.exp(own_score - highest)
    denominator = jnp.sum(expo_cache, axis=-1) + expo_new
    weights = (expo_cache / denominator[..., None]).astype(jnp.bfloat16)
    weight_new = (expo_new / denominator).astype(jnp.bfloat16)
    summed = jnp.einsum("skgj,sjkd->skgd", weights, value_heads, preferred_element_type=jnp.float32)
    summed = summed + weight_new.astype(jnp.float32)[..., None] * new_values
    return summed.reshape(slots, HEADS * DH).astype(jnp.bfloat16)


def local(
    remaining_states,
    scaling_factor_vector,
    probe_projection_matrix,
    memory_projection_matrix,
    final_projection_matrix,
    memorized_address_tensor,
    memorized_content_tensor,
    retained_sequence_ids,
    occupied_positions,
):
    group_size = lax.axis_size(GX)
    local_ordinal = lax.axis_index(GX)
    sequence_count_local = memorized_address_tensor.shape[0]
    complete_sequence_set = sequence_count_local * group_size
    retained_ordinal = (
        retained_sequence_ids[:, None]
        == jnp.arange(complete_sequence_set, dtype=jnp.int32)[None, :]
    ).astype(jnp.bfloat16)
    normed_all = lax.all_gather(
        normalize(remaining_states, scaling_factor_vector), GX, axis=0, tiled=True
    )
    probe_vectors = jnp.dot(
        normed_all, probe_projection_matrix, preferred_element_type=jnp.float32
    ).astype(jnp.bfloat16)
    width_dev = memory_projection_matrix.shape[0]
    normed_cols = lax.dynamic_slice_in_dim(normed_all, local_ordinal * width_dev, width_dev, 1)
    kv_part = jnp.dot(normed_cols, memory_projection_matrix, preferred_element_type=jnp.float32)
    slot_select = jnp.transpose(retained_ordinal).astype(jnp.float32)
    sliced = slot_select
    new_kv = sum_by_axis(
        jnp.dot(sliced, kv_part, precision=lax.Precision.HIGHEST), GX, (1, 0), 0
    ).astype(jnp.bfloat16)
    query_slots = jnp.einsum(
        "wa,wy->ay", retained_ordinal, probe_vectors, preferred_element_type=jnp.float32
    ).astype(jnp.bfloat16)
    owner_queries = lax.all_to_all(query_slots, GX, split_axis=0, concat_axis=1, tiled=True)
    attended = attend_slots(
        owner_queries,
        new_kv,
        memorized_address_tensor,
        memorized_content_tensor,
        occupied_positions,
    )
    final_result = lax.all_to_all(attended, GX, split_axis=1, concat_axis=0, tiled=True)
    contextual_states = jnp.dot(
        retained_ordinal, final_result, preferred_element_type=jnp.float32
    ).astype(jnp.bfloat16)
    sliced = contextual_states
    projected = sum_by_axis(
        jnp.dot(sliced, final_projection_matrix, preferred_element_type=jnp.float32), GX, (1, 0), 0
    )
    return (remaining_states.astype(jnp.float32) + projected).astype(jnp.bfloat16)


def solution(mesh):
    torus = Mesh(mesh.devices.reshape(mesh.shape["grp"], 16, 2), ("grp", "gx_0", "gx_1"))
    placed = (
        P(GRP_GX, None),
        P(),
        P(None, GX),
        P(GX, None),
        P(GX, None),
        P(GRP_GX, None, None),
        P(GRP_GX, None, None),
        P("grp"),
        P(GRP_GX),
    )
    return jax.shard_map(
        local, mesh=torus, in_specs=placed, out_specs=P(GRP_GX, None), check_vma=False
    )
```

profile of v0, /device:TPU:69, one launch (start us, length us, event | category | flops | bytes accessed | tf_op | source)
XLA Modules:
  0.0 479.7 jit_solution(11570410247715035204)
XLA Ops:
  6.5 0.0 copy-start
  6.6 0.0 all-gather.3.cloned.1.call-start
  6.6 0.9 convert_element_type.60
  7.4 1.2 fusion.25
  8.6 1.7 fusion.33
  10.3 0.1 all-gather.3.cloned.1.call-update
  10.3 0.1 reduce-scatter.3.cloned.1.call-start
  10.4 0.0 copy-start.3
  10.4 77.6 %all-gather.3.cloned.1.call-done = bf16[32,4,16384]{2,1,0:T(4,128)(2,1)} async-done(((bf16[1,4,16384]{2,1,0:T(4,128)(2,1)}), bf16[32,4,16384]{2,1,0:T(4,128)(2,1)}) %all-gather.3.cloned.1.call-update) | async-done | bytes 4194320 | tf_op jit(solution)/shard_map/all_gather | solution.py:91
  88.1 6.9 %reshape.89 = bf16[128,16384]{1,0:T(8,128)(2,1)} reshape(bf16[32,4,16384]{2,1,0:T(4,128)(2,1)} %all-gather.3.cloned.1.call-done) | data formatting | bytes 8388608
  95.0 0.0 copy-done
  95.0 1.2 fusion.34
  96.2 0.0 copy-done.3
  96.2 1.9 fusion.23
  98.1 2.3 copy.22
  100.4 0.1 reduce-scatter.3.cloned.1.call-update
  100.5 0.1 reduce-scatter.5.cloned.1.call-start
  100.5 16.9 %reduce-scatter.3.cloned.1.call-done = f32[16,32,1024]{2,1,0:T(8,128)} async-done(((f32[32,32,1024]{2,1,0:T(8,128)}), f32[16,32,1024]{2,1,0:T(8,128)}) %reduce-scatter.3.cloned.1.call-update) | async-done | bytes 2097168 | tf_op jit(solution)/shard_map/reduce_scatter | solution.py:24
  117.5 0.1 reduce-scatter.5.cloned.1.call-update
  117.5 0.0 copy-start.4
  117.5 7.2 %convolution_convert_fusion = bf16[1024,256]{1,0:T(8,128)(2,1)} fusion(bf16[128,16384]{1,0:T(8,128)(2,1)} %reshape.89, bf16[16384,256]{1,0:T(8,128)(2,1)} %param.11, s32[128]{0:T(128)S(1)} %copy-done.3), kind=kOutput, calls=%fused_computation.10 | convolution fusion | flops 1141276672 | bytes 13107712 | tf_op jit(solution)/shard_map/wa,wy->ay/dot_general | solution.py:105
  124.8 12.3 %all-to-all-start = ((bf16[32,32,256]{2,1,0:T(8,128)(2,1)}), bf16[32,32,256]{2,1,0:T(8,128)(2,1)S(1)}, u32[]{:S(2)}, u32[]{:S(2)}) async-start(bf16[32,32,256]{2,1,0:T(8,128)(2,1)} %bitcast.1), calls=%async_computation | async-start | bytes 1048576 | tf_op jit(solution)/shard_map/all_to_all | solution.py:108
  137.1 0.1 all-reduce.5.cloned.1.call-start
  137.2 0.0 copy-done.4
  137.2 0.1 iota_compare_fusion.5
  137.3 36.1 %all-to-all-done = bf16[32,32,256]{2,1,0:T(8,128)(2,1)S(1)} async-done(((bf16[32,32,256]{2,1,0:T(8,128)(2,1)}), bf16[32,32,256]{2,1,0:T(8,128)(2,1)S(1)}, u32[]{:S(2)}, u32[]{:S(2)}) %all-to-all-start) | async-done | bytes 524320 | tf_op jit(solution)/shard_map/all_to_all | solution.py:108
  173.4 0.3 copy.20
  173.7 0.2 reshape.81
  173.9 4.6 fusion.40
  178.5 19.6 %reduce-scatter.5.cloned.1.call-done = f32[1,32,1024]{2,1,0:T(8,128)} async-done(((f32[16,32,1024]{2,1,0:T(8,128)}), f32[1,32,1024]{2,1,0:T(8,128)}) %reduce-scatter.5.cloned.1.call-update) | async-done | bytes 131088 | tf_op jit(solution)/shard_map/reduce_scatter | solution.py:24
  198.1 0.9 convert_bitcast_fusion
  199.0 0.4 multiply_reduce_fusion
  199.5 0.7 fusion.19
  200.2 0.1 fusion.37
  200.3 3.5 fusion.15
  203.7 0.2 convert_element_type.71
  203.9 0.3 copy.24
  204.2 51.2 %all_to_all.32 = bf16[32,32,256]{2,0,1:T(8,128)(2,1)S(1)} all-to-all(bf16[32,32,256]{2,0,1:T(8,128)(2,1)S(1)} %copy.24), channel_id=1, replica_groups=mesh['grp'=4,'gx_0'=16,'gx_1'=2] {'gx_0','gx_1'}, dimensions={1} | all-to-all | bytes 1048576 | tf_op jit(solution)/shard_map/all_to_all | solution.py:116
  255.4 8.2 %fusion.18 = f32[128,16384]{1,0:T(8,128)} fusion(bf16[256,16384]{1,0:T(8,128)(2,1)} %param.13, bf16[1024,256]{1,0:T(8,128)(2,1)S(1)} %bitcast.58, s32[128]{0:T(128)S(1)} %copy-done.3), kind=kOutput, calls=%fused_computation.13 | convolution fusion | flops 1141014528 | bytes 17302016 | tf_op jit(solution)/shard_map/dot_general | solution.py:122
  263.6 9.8 %reshape_reshape.7 = f32[16,2,4,16384]{3,2,1,0:T(4,128)} reshape(f32[128,16384]{1,0:T(8,128)} %fusion.18) | data formatting | bytes 16777216 | tf_op jit(solution)/shard_map/reshape;reshape | solution.py:20
  273.4 7.5 %copy.25 = f32[2,16,4,16384]{3,2,1,0:T(4,128)} copy(f32[2,16,4,16384]{3,2,0,1:T(4,128)} %bitcast.55) | data formatting | bytes 16777216 | tf_op jit(solution)/shard_map/transpose | solution.py:21
  280.9 0.0 copy-start.6
  280.9 0.1 all-reduce.5.cloned.1.call-update
  281.0 0.1 all-reduce.7.cloned.1.call-start
  281.1 0.5 copy-done.6
  281.6 0.6 dynamic-slice
  282.8 42.3 %all-reduce.5.cloned.1.call-done = f32[32,4,16384]{2,1,0:T(4,128)} async-done(((f32[32,4,16384]{2,1,0:T(4,128)}), f32[32,4,16384]{2,1,0:T(4,128)}) %all-reduce.5.cloned.1.call-update) | async-done | bytes 8388624
  325.1 0.0 copy-start.1
  325.1 4.6 constant_dynamic-slice_fusion
  329.8 0.0 copy-start.5
  329.8 0.0 copy-start.2
  329.8 0.1 all-reduce.7.cloned.1.call-update
  329.8 0.6 copy-done.5
  330.4 0.6 dynamic-slice.2
  331.0 140.0 %all-reduce.7.cloned.1.call-done = f32[16,4,16384]{2,1,0:T(4,128)} async-done(((f32[16,4,16384]{2,1,0:T(4,128)}), f32[16,4,16384]{2,1,0:T(4,128)}) %all-reduce.7.cloned.1.call-update) | async-done | bytes 4194320
  471.0 0.0 copy-done.2
  471.0 2.2 fusion.28
  473.2 0.0 copy-done.1
  (5 shorter events, 0.1 us)
Async XLA Ops:
  6.5 88.4 %copy-start = (bf16[512,1024]{1,0:T(8,128)(2,1)S(1)}, bf16[512,1024]{1,0:T(8,128)(2,1)}, u32[]{:S(2)}) copy-start(bf16[512,1024]{1,0:T(8,128)(2,1)} %param.12) | copy-start | bytes 3145732
  6.6 81.5 %all-gather.3.cloned.1.call-start = ((), (), s32[]{:S(2)}) async-start(), calls=%async_computation.6 | async-start | bytes 4325376 | tf_op jit(solution)/shard_map/all_gather | solution.py:91
  10.3 107.1 %reduce-scatter.3.cloned.1.call-start = ((), (), s32[]{:S(2)}) async-start(), calls=%async_computation.4 | async-start | bytes 6291456 | tf_op jit(solution)/shard_map/reduce_scatter | solution.py:24
  10.4 85.8 %copy-start.3 = (s32[128]{0:T(128)S(1)}, s32[128]{0:T(128)}, u32[]{:S(2)}) copy-start(s32[128]{0:T(128)} %param.16) | copy-start | bytes 1540
  100.5 97.6 %reduce-scatter.5.cloned.1.call-start = ((), (), s32[]{:S(2)}) async-start(), calls=%async_computation.5 | async-start | bytes 2228224 | tf_op jit(solution)/shard_map/reduce_scatter | solution.py:24
  117.5 19.7 %copy-start.4 = (s32[32]{0:T(128)S(1)}, s32[32]{0:T(128)}, u32[]{:S(2)}) copy-start(s32[32]{0:T(128)} %param.17) | copy-start | bytes 388
  124.8 48.6 %all-to-all-start = ((bf16[32,32,256]{2,1,0:T(8,128)(2,1)}), bf16[32,32,256]{2,1,0:T(8,128)(2,1)S(1)}, u32[]{:S(2)}, u32[]{:S(2)}) async-start(bf16[32,32,256]{2,1,0:T(8,128)(2,1)} %bitcast.1), calls=%async_computation | async-start | bytes 1048576 | tf_op jit(solution)/shard_map/all_to_all | solution.py:108
  137.1 188.0 %all-reduce.5.cloned.1.call-start = ((), (), s32[]{:S(2)}) async-start(), calls=%async_computation.7 | async-start | bytes 16777216
  280.9 0.7 copy-start.6
  281.0 190.0 %all-reduce.7.cloned.1.call-start = ((), (), s32[]{:S(2)}) async-start(), calls=%async_computation.8 | async-start | bytes 8388608
  325.1 148.1 %copy-start.1 = (bf16[512,1024]{1,0:T(8,128)(2,1)S(1)}, bf16[512,1024]{1,0:T(8,128)(2,1)}, u32[]{:S(2)}) copy-start(bf16[512,1024]{1,0:T(8,128)(2,1)} %param.12) | copy-start | bytes 3145732
  329.8 0.7 copy-start.5
  329.8 141.2 %copy-start.2 = (bf16[4,16384]{1,0:T(4,128)(2,1)S(1)}, bf16[4,16384]{1,0:T(4,128)(2,1)}, u32[]{:S(2)}) copy-start(bf16[4,16384]{1,0:T(4,128)(2,1)} %param.9) | copy-start | bytes 393220
Sparse Core Ops, SparseCore 0:
  10.4 77.5 all-gather.2
  100.6 16.8 reduce-scatter.2
  119.9 78.1 reduce-scatter.4
  281.1 43.9 all-reduce.4
  329.9 140.9 all-reduce.6
where the time goes:
time: 489 us; the launch traced here: 480 us
  waiting for transfers between devices  333 us (68%)
  blocking collectives  51.2 us (10%)
  local copies, waits for them, and re-layouts  34.4 us (7%)
  matrix products  26.6 us (5%)
  between operations  14 us (3%)
  starting transfers between devices  12.6 us (3%)
  other arithmetic  8.13 us (2%)
    unnamed x7, waiting for transfers between devices  183 us
    all_gather x1, waiting for transfers between devices, local(): lax.all_gather(normalize(remaining_states, scaling_factor_vector), GX, ax...  77.6 us
    all_to_all x1, blocking collectives, local(): lax.all_to_all(attended, GX, split_axis=1, concat_axis=0, tiled=True)  51.2 us
    reduce_scatter x2, waiting for transfers between devices, sum_in_order(): pieces = lax.psum_scatter(pieces, axes[k], scatter_dimension=0, tiled=True)  36.5 us
    all_to_all x1, waiting for transfers between devices, local(): lax.all_to_all(query_slots, GX, split_axis=0, concat_axis=1, tiled=True)  36.1 us
    unnamed x18, local copies, waits for them, and re-layouts  13.8 us
    all_to_all x1, starting transfers between devices, local(): lax.all_to_all(query_slots, GX, split_axis=0, concat_axis=1, tiled=True)  12.3 us
    another operation x2, local copies, waits for them, and re-layouts, sum_in_order(): pieces = pieces.reshape(*lengths, *pieces.shape[1:])  12.1 us
  transfers between devices with their start and end apart: 6, of which 6 were waited for; matrix products, arithmetic and copies ran while one was open for 3% of the time, Pallas kernels for 0%

commit v1 on v0

v1 whole, which is shorter than its diff:
```python
import functools
import math

import jax
import jax.numpy as jnp
from jax import lax
from jax.experimental import pallas as pl
from jax.experimental.pallas import tpu as pltpu
from jax.sharding import PartitionSpec as P

HEADS = 64
KV = 4
DH = 128
EPS = 1e-05
MESH = pl.DeviceIdType.MESH
F32 = jnp.float32
BF16 = jnp.bfloat16


class Place:
    def __init__(self, n):
        self.n = n
        self.chips = n // 2
        self.me = lax.axis_index("gx")
        self.c = lax.rem(self.me, 2)
        self.z = lax.div(self.me, 2)
        self.up = lax.rem(self.me + 2, n)
        self.dn = lax.rem(self.me + n - 2, n)
        self.sib = self.me + 1 - 2 * self.c

    def chip(self, offset):
        return lax.rem(self.z + offset + 2 * self.chips, self.chips)

    def greet(self):
        barrier = pltpu.get_barrier_semaphore()
        for other in (self.up, self.dn, self.sib):
            pl.semaphore_signal(barrier, inc=1, device_id={"gx": other}, device_id_type=MESH)
        pl.semaphore_wait(barrier, 3)


def remote(src, dst, send_sem, recv_sem, device):
    return pltpu.make_async_remote_copy(
        src_ref=src,
        dst_ref=dst,
        send_sem=send_sem,
        recv_sem=recv_sem,
        device_id={"gx": device},
        device_id_type=MESH,
    )


def wait_bytes(ref, sem):
    pltpu.make_async_copy(ref, ref, sem).wait()


def gather_kernel(
    n,
    nj,
    nq,
    states,
    gain,
    wq_hbm,
    wkv_hbm,
    qall,
    kvall,
    xs,
    x32,
    nb,
    wq,
    wkv,
    acc,
    kvp,
    kvs,
    kvu,
    kvd,
    w_sem,
    x_sem,
    a_send,
    a_ru,
    a_rd,
    a_fs,
    a_fr,
    q_send,
    q_ru,
    q_rd,
    q_fs,
    q_fr,
    s_sem,
    r_send,
    r_ru,
    r_rd,
    g_send,
    g_ru,
    g_rd,
    g_fs,
    g_fr,
):
    p = Place(n)
    me, c, z = p.me, p.c, p.z
    chips = p.chips
    ups, dns = chips // 2, chips - 1 - chips // 2
    d = states.shape[1]
    kc = d // (2 * nj)

    wq_copy = pltpu.make_async_copy(wq_hbm, wq, w_sem.at[0])
    wkv_copy = pltpu.make_async_copy(wkv_hbm, wkv, w_sem.at[1])
    wq_copy.start()
    wkv_copy.start()

    p.greet()
    raw = remote(states, xs, x_sem.at[0], x_sem.at[1], p.sib)
    raw.start()
    raw.wait()

    first = c == 0
    total = jnp.zeros((8, 1), F32)
    for k in range(2 * nj):
        cols = pl.ds(k * kc, kc)
        own = states[:, cols].astype(F32)
        other = xs[:, cols].astype(F32)
        rows = jnp.concatenate(
            [jnp.where(first, own, other), jnp.where(first, other, own)], axis=0
        )
        x32[:, cols] = rows
        total = total + jnp.sum(rows * rows, axis=1, keepdims=True)
    inverse = lax.rsqrt(total / d + EPS)
    for k in range(2 * nj):
        cols = pl.ds(k * kc, kc)
        nb[k, z] = (x32[:, cols] * inverse * gain[:, cols].astype(F32)).astype(BF16)

    def a_part(j, origin):
        return nb.at[c * nj + j, origin]

    def a_up(t, j):
        ref = a_part(j, p.chip(1 - t))
        return remote(ref, ref, a_send.at[0, j], a_ru.at[t - 1, j], p.up)

    def a_dn(t, j):
        ref = a_part(j, p.chip(t - 1))
        return remote(ref, ref, a_send.at[1, j], a_rd.at[t - 1, j], p.dn)

    def a_forward(j, origin):
        ref = a_part(j, origin)
        remote(ref, ref, a_fs.at[j], a_fr.at[j], p.sib).start()

    def a_take_up(t, j):
        ref = a_part(j, p.chip(-t))
        remote(ref, ref, a_send.at[0, j], a_ru.at[t - 1, j], p.up).wait_recv()

    def a_take_dn(t, j):
        ref = a_part(j, p.chip(t))
        remote(ref, ref, a_send.at[1, j], a_rd.at[t - 1, j], p.dn).wait_recv()

    for j in range(nj):
        a_up(1, j).start()
        a_dn(1, j).start()

    def a_step(t, carry):
        for j in range(nj):
            a_take_up(t - 1, j)
            a_up(t, j).start()
            a_take_dn(t - 1, j)
            a_dn(t, j).start()
            a_forward(j, p.chip(1 - t))
            a_forward(j, p.chip(t - 1))
        return carry

    lax.fori_loop(2, dns + 1, a_step, 0)
    for j in range(nj):
        a_take_up(ups - 1, j)
        a_up(ups, j).start()
        a_take_dn(dns, j)
        a_forward(j, p.chip(1 - ups))
        a_forward(j, p.chip(dns))

    wq_copy.wait()
    wkv_copy.wait()

    def q_part(k):
        lhs = nb[k].reshape(8 * chips, kc)
        rhs = wq[pl.ds(pl.multiple_of(k * kc, kc), kc), :]
        return jnp.dot(lhs, rhs, preferred_element_type=F32)

    for j in range(nj):
        a_take_up(ups, j)
        a_forward(j, p.chip(-ups))
        part = q_part(c * nj + j)
        acc[...] = part if j == 0 else acc[...] + part
    for j in range(nj):
        k = (1 - c) * nj + j
        wait_bytes(nb.at[k, pl.ds(0, chips - 1)], a_fr.at[j])
        acc[...] += q_part(k)

    width = wkv.shape[0]
    per = kc // width
    k_own = lax.div(me, per)
    off = pl.multiple_of(lax.rem(me, per) * width, width)
    lhs = nb[k_own, :, :, pl.ds(off, width)].reshape(8 * chips, width)
    half = wkv.shape[1] // 2
    for h in range(2):
        kvp[h] = jnp.dot(
            lhs, wkv[:, h * half : (h + 1) * half], preferred_element_type=F32
        ).reshape(chips, 8, half)
    qall[me] = acc[...].astype(BF16)

    rows = 8 * chips // nq

    def q_block(j, origin):
        return qall.at[2 * origin + c, pl.ds(j * rows, rows)]

    def q_up(t, j):
        ref = q_block(j, p.chip(1 - t))
        return remote(ref, ref, q_send.at[0, j], q_ru.at[t - 1, j], p.up)

    def q_dn(t, j):
        ref = q_block(j, p.chip(t - 1))
        return remote(ref, ref, q_send.at[1, j], q_rd.at[t - 1, j], p.dn)

    def q_take_up(t, j):
        ref = q_block(j, p.chip(-t))
        remote(ref, ref, q_send.at[0, j], q_ru.at[t - 1, j], p.up).wait_recv()

    def q_take_dn(t, j):
        ref = q_block(j, p.chip(t))
        remote(ref, ref, q_send.at[1, j], q_rd.at[t - 1, j], p.dn).wait_recv()

    def q_forward(j, origin):
        ref = q_block(j, origin)
        remote(ref, ref, q_fs.at[j], q_fr.at[j], p.sib).start()

    for j in range(nq):
        q_up(1, j).start()
        q_dn(1, j).start()
    swap = remote(kvp.at[1 - c], kvs, s_sem.at[0], s_sem.at[1], p.sib)
    swap.start()
    for j in range(nq):
        q_forward(j, z)
    swap.wait_recv()

    def r_up(t):
        return remote(kvu.at[t - 1], kvu.at[t], r_send.at[0, t - 1], r_ru.at[t - 1], p.up)

    def r_dn(t):
        return remote(kvd.at[t - 1], kvd.at[t], r_send.at[1, t - 1], r_rd.at[t - 1], p.dn)

    def kv_own(chip):
        return kvp[c, chip] + kvs[chip]

    kvu[0] = kv_own(p.chip(ups))
    r_up(1).start()
    kvd[0] = kv_own(p.chip(-dns))
    r_dn(1).start()

    def r_up_step(t):
        r_up(t - 1).wait_recv()
        kvu[t - 1] += kv_own(p.chip(ups + 1 - t))
        r_up(t).start()

    def r_dn_step(t):
        r_dn(t - 1).wait_recv()
        kvd[t - 1] += kv_own(p.chip(t - 1 - dns))
        r_dn(t).start()

    def q_step(t, carry):
        for j in range(nq):
            q_take_up(t - 1, j)
            q_up(t, j).start()
            q_take_dn(t - 1, j)
            q_dn(t, j).start()
        r_up_step(t)
        r_dn_step(t)
        for j in range(nq):
            q_forward(j, p.chip(1 - t))
            q_forward(j, p.chip(t - 1))
        return carry

    lax.fori_loop(2, dns + 1, q_step, 0)
    for j in range(nq):
        q_take_up(ups - 1, j)
        q_up(ups, j).start()
        q_take_dn(dns, j)
    r_up_step(ups)
    for j in range(nq):
        q_forward(j, p.chip(1 - ups))
        q_forward(j, p.chip(dns))
    r_dn(dns).wait_recv()
    r_up(ups).wait_recv()
    kvall[c, z] = (kvu[ups] + kvd[dns] + kv_own(z)).astype(BF16)

    def g_part(origin):
        return kvall.at[c, origin]

    def g_up(t):
        ref = g_part(p.chip(1 - t))
        return remote(ref, ref, g_send.at[0], g_ru.at[t - 1], p.up)

    def g_dn(t):
        ref = g_part(p.chip(t - 1))
        return remote(ref, ref, g_send.at[1], g_rd.at[t - 1], p.dn)

    def g_take_up(t):
        ref = g_part(p.chip(-t))
        remote(ref, ref, g_send.at[0], g_ru.at[t - 1], p.up).wait_recv()

    def g_take_dn(t):
        ref = g_part(p.chip(t))
        remote(ref, ref, g_send.at[1], g_rd.at[t - 1], p.dn).wait_recv()

    def g_forward(origin):
        ref = g_part(origin)
        remote(ref, ref, g_fs.at[0], g_fr.at[0], p.sib).start()

    g_up(1).start()
    g_dn(1).start()
    g_forward(z)
    for j in range(nq):
        q_take_up(ups, j)
        q_forward(j, p.chip(-ups))

    def g_step(t, carry):
        g_take_up(t - 1)
        g_up(t).start()
        g_take_dn(t - 1)
        g_dn(t).start()
        g_forward(p.chip(1 - t))
        g_forward(p.chip(t - 1))
        return carry

    lax.fori_loop(2, dns + 1, g_step, 0)
    g_take_up(ups - 1)
    g_up(ups).start()
    g_take_dn(dns)
    g_forward(p.chip(1 - ups))
    g_forward(p.chip(dns))
    g_take_up(ups)
    g_forward(p.chip(-ups))

    for j in range(nj):
        wait_bytes(nb.at[0, pl.ds(0, ups)], a_send.at[0, j])
        wait_bytes(nb.at[0, pl.ds(0, dns)], a_send.at[1, j])
        wait_bytes(nb.at[0, pl.ds(0, chips - 1)], a_fs.at[j])
    for j in range(nq):
        wait_bytes(qall.at[pl.ds(0, ups), pl.ds(0, rows)], q_send.at[0, j])
        wait_bytes(qall.at[pl.ds(0, dns), pl.ds(0, rows)], q_send.at[1, j])
        wait_bytes(qall.at[pl.ds(0, chips), pl.ds(0, rows)], q_fs.at[j])
        wait_bytes(qall.at[pl.ds(0, chips), pl.ds(0, rows)], q_fr.at[j])
    swap.wait_send()

    def r_sent(t, carry):
        r_up(t).wait_send()
        r_dn(t).wait_send()
        return carry

    lax.fori_loop(1, dns + 1, r_sent, 0)
    r_up(ups).wait_send()
    wait_bytes(kvall.at[0, pl.ds(0, ups)], g_send.at[0])
    wait_bytes(kvall.at[0, pl.ds(0, dns)], g_send.at[1])
    wait_bytes(kvall.at[0], g_fs.at[0])
    wait_bytes(kvall.at[0], g_fr.at[0])


def gather(states, gain, wq, wkv, n):
    r, d = states.shape
    nj, nq = 4, 2
    chips = n // 2
    ups, dns = chips // 2, chips - 1 - chips // 2
    rows = 8 * chips
    width = wq.shape[1]
    half = wkv.shape[1] // 2
    dma = pltpu.SemaphoreType.DMA
    vmem = pltpu.VMEM
    return pl.pallas_call(
        functools.partial(gather_kernel, n, nj, nq),
        name="gather_queries",
        out_shape=(
            jax.ShapeDtypeStruct((n, rows, width), BF16),
            jax.ShapeDtypeStruct((2, chips, 8, half), BF16),
        ),
        in_specs=[pl.BlockSpec(memory_space=pltpu.VMEM)] * 2
        + [pl.BlockSpec(memory_space=pl.ANY)] * 2,
        out_specs=(pl.BlockSpec(memory_space=pltpu.VMEM),) * 2,
        scratch_shapes=[
            vmem((r, d), BF16),
            vmem((2 * r, d), F32),
            vmem((2 * nj, chips, 2 * r, d // (2 * nj)), BF16),
            vmem(wq.shape, BF16),
            vmem(wkv.shape, BF16),
            vmem((rows, width), F32),
            vmem((2, chips, 8, half), F32),
            vmem((chips, 8, half), F32),
            vmem((ups + 1, 8, half), F32),
            vmem((dns + 1, 8, half), F32),
            dma((2,)),
            dma((2,)),
            dma((2, nj)),
            dma((ups, nj)),
            dma((dns, nj)),
            dma((nj,)),
            dma((nj,)),
            dma((2, nq)),
            dma((ups, nq)),
            dma((dns, nq)),
            dma((nq,)),
            dma((nq,)),
            dma((2,)),
            dma((2, ups)),
            dma((ups,)),
            dma((dns,)),
            dma((2,)),
            dma((ups,)),
            dma((dns,)),
            dma((1,)),
            dma((1,)),
        ],
        compiler_params=pltpu.CompilerParams(collective_id=0, has_side_effects=True),
    )(states, gain, wq, wkv)


def attend_kernel(
    ids_s,
    occ_s,
    ids_row,
    ids_col,
    qall,
    kvall,
    k_hbm,
    v_hbm,
    out,
    slots_s,
    kbuf,
    vbuf,
    qs,
    att,
    new,
    k_sem,
    v_sem,
):
    slots, cache, _ = k_hbm.shape
    n, rows, width = qall.shape
    base = lax.axis_index("gx") * slots
    per = width // DH
    group = HEADS // KV

    def find(r, count):
        b = ids_s[r] - base
        mine = (b >= 0) & (b < slots)

        @pl.when(mine)
        def _():
            slots_s[count] = b
            pltpu.make_async_copy(k_hbm.at[b], kbuf.at[count], k_sem.at[count]).start()
            pltpu.make_async_copy(v_hbm.at[b], vbuf.at[count], v_sem.at[count]).start()

        return count + mine.astype(jnp.int32)

    count = lax.fori_loop(0, rows, find, jnp.int32(0))

    pick = (
        ids_row[...] - base == lax.broadcasted_iota(jnp.int32, (slots, rows), 0)
    ).astype(BF16)
    put = (
        ids_col[...] - base == lax.broadcasted_iota(jnp.int32, (rows, slots), 1)
    ).astype(BF16)
    for i in range(n):
        picked = jnp.dot(pick, qall[i], preferred_element_type=F32)
        for h in range(per):
            row = (i * per + h) * slots
            qs[row : row + slots, :] = picked[:, h * DH : (h + 1) * DH]
    for h in range(2):
        new[h] = jnp.dot(pick, kvall[h], preferred_element_type=F32)
    att[...] = jnp.zeros_like(att)

    scale = 1.0 / math.sqrt(DH)

    def one(i, carry):
        s = slots_s[i]
        filled = occ_s[s]
        pltpu.make_async_copy(k_hbm.at[0], kbuf.at[i], k_sem.at[i]).wait()
        pltpu.make_async_copy(v_hbm.at[0], vbuf.at[i], v_sem.at[i]).wait()
        q = qs[pl.ds(s, HEADS, stride=slots), :]
        q16 = q.astype(BF16)
        k_new = new[0, pl.ds(s, 1), :]
        v_new = new[1, pl.ds(s, 1), :]
        scores, own = [], []
        for g in range(KV):
            cols = slice(g * DH, (g + 1) * DH)
            head = slice(g * group, (g + 1) * group)
            scores.append(
                lax.dot_general(
                    q16[head],
                    kbuf[i, :, cols],
                    (((1,), (1,)), ((), ())),
                    preferred_element_type=F32,
                )
            )
            own.append(jnp.sum(q[head] * k_new[:, cols], axis=1, keepdims=True))
        scores = jnp.concatenate(scores, axis=0) * scale
        own = jnp.concatenate(own, axis=0) * scale
        visible = lax.broadcasted_iota(jnp.int32, (HEADS, cache), 1) < filled
        scores = jnp.where(visible, scores, -1e30)
        highest = jnp.maximum(jnp.max(scores, axis=1, keepdims=True), own)
        expo = jnp.where(visible, jnp.exp(scores - highest), 0.0)
        expo_new = jnp.exp(own - highest)
        denominator = jnp.sum(expo, axis=1, keepdims=True) + expo_new
        weights = (expo / denominator).astype(BF16)
        weight_new = (expo_new / denominator).astype(BF16).astype(F32)
        summed = []
        for g in range(KV):
            cols = slice(g * DH, (g + 1) * DH)
            head = slice(g * group, (g + 1) * group)
            part = jnp.dot(weights[head], vbuf[i, :, cols], preferred_element_type=F32)
            summed.append(part + weight_new[head] * v_new[:, cols])
        att[pl.ds(s, HEADS, stride=slots), :] = jnp.concatenate(summed, axis=0)
        return carry

    lax.fori_loop(0, count, one, 0)

    for i in range(n):
        block = jnp.concatenate(
            [
                att[(i * per + h) * slots : (i * per + h + 1) * slots, :].astype(BF16)
                for h in range(per)
            ],
            axis=1,
        )
        out[i] = jnp.dot(put, block, preferred_element_type=F32).astype(BF16)


def attend(ids, occ, qall, kvall, keys, values):
    n, rows, width = qall.shape
    slots, cache, lanes = keys.shape
    vm = pl.BlockSpec(memory_space=pltpu.VMEM)
    sm = pl.BlockSpec(memory_space=pltpu.SMEM)
    hbm = pl.BlockSpec(memory_space=pl.ANY)
    return pl.pallas_call(
        attend_kernel,
        name="attend_slots",
        out_shape=jax.ShapeDtypeStruct((n, rows, width), BF16),
        in_specs=[sm, sm, vm, vm, vm, vm, hbm, hbm],
        out_specs=vm,
        scratch_shapes=[
            pltpu.SMEM((slots + 1,), jnp.int32),
            pltpu.VMEM((slots, cache, lanes), BF16),
            pltpu.VMEM((slots, cache, lanes), BF16),
            pltpu.VMEM((HEADS * slots, DH), F32),
            pltpu.VMEM((HEADS * slots, DH), F32),
            pltpu.VMEM((2, slots, lanes), F32),
            pltpu.SemaphoreType.DMA((slots,)),
            pltpu.SemaphoreType.DMA((slots,)),
        ],
    )(ids, occ, ids.reshape(1, rows), ids.reshape(rows, 1), qall, kvall, keys, values)


def project_kernel(
    n,
    nd,
    nj,
    states,
    parts,
    wo_hbm,
    out,
    wo,
    sb,
    du,
    dd,
    mix,
    mine,
    theirs,
    heard,
    eu,
    ed,
    tail,
    tail_in,
    w_sem,
    b_send,
    b_recv,
    d_send,
    d_ru,
    d_rd,
    h_send,
    h_recv,
    e_send,
    e_ru,
    e_rd,
    t_send,
    t_recv,
):
    p = Place(n)
    c, z = p.c, p.z
    chips = p.chips
    ups, dns = chips // 2, chips - 1 - chips // 2
    d = states.shape[1]
    kc = d // (2 * nj)

    wo_copy = pltpu.make_async_copy(wo_hbm, wo, w_sem.at[0])
    wo_copy.start()
    p.greet()

    def b_copy(offset):
        chip = p.chip(offset)
        index = lax.rem(offset + chips, chips)
        return remote(
            parts.at[2 * chip + 1 - c], sb.at[chip], b_send.at[0], b_recv.at[index], p.sib
        )

    def b_take(offset):
        chip = p.chip(offset)
        index = lax.rem(offset + chips, chips)
        remote(
            parts.at[2 * chip + c], sb.at[chip], b_send.at[0], b_recv.at[index], p.sib
        ).wait_recv()

    def b_start(t, carry):
        b_copy(ups + 1 - t).start()
        b_copy(t - 1 - dns).start()
        return carry

    lax.fori_loop(1, dns + 1, b_start, 0)
    b_copy(jnp.int32(1)).start()
    b_copy(jnp.int32(0)).start()

    rows = 8 * chips // nd

    def d_up(t, j):
        part = pl.ds(j * rows, rows)
        return remote(
            du.at[t - 1, part], du.at[t, part], d_send.at[0, j], d_ru.at[t - 1, j], p.up
        )

    def d_dn(t, j):
        part = pl.ds(j * rows, rows)
        return remote(
            dd.at[t - 1, part], dd.at[t, part], d_send.at[1, j], d_rd.at[t - 1, j], p.dn
        )

    def d_own(chip, j):
        part = pl.ds(j * rows, rows)
        return parts[2 * chip + c, part, :] + sb[chip, part, :]

    b_take(jnp.int32(ups))
    for j in range(nd):
        du[0, pl.ds(j * rows, rows)] = d_own(p.chip(ups), j)
        d_up(1, j).start()
    b_take(jnp.int32(-dns))
    for j in range(nd):
        dd[0, pl.ds(j * rows, rows)] = d_own(p.chip(-dns), j)
        d_dn(1, j).start()

    def d_up_step(t):
        b_take(ups + 1 - t)
        for j in range(nd):
            d_up(t - 1, j).wait_recv()
            du[t - 1, pl.ds(j * rows, rows)] += d_own(p.chip(ups + 1 - t), j)
            d_up(t, j).start()

    def d_both_step(t, carry):
        b_take(ups + 1 - t)
        b_take(t - 1 - dns)
        for j in range(nd):
            part = pl.ds(j * rows, rows)
            d_up(t - 1, j).wait_recv()
            du[t - 1, part] += d_own(p.chip(ups + 1 - t), j)
            d_up(t, j).start()
            d_dn(t - 1, j).wait_recv()
            dd[t - 1, part] += d_own(p.chip(t - 1 - dns), j)
            d_dn(t, j).start()
        return carry

    lax.fori_loop(2, dns + 1, d_both_step, 0)
    d_up_step(jnp.int32(ups))
    b_take(jnp.int32(0))
    for j in range(nd):
        part = pl.ds(j * rows, rows)
        d_dn(dns, j).wait_recv()
        d_up(ups, j).wait_recv()
        mix[part] = du[ups, part] + dd[dns, part] + d_own(z, j)
    attended = mix[...]
    wo_copy.wait()

    def product(half, j):
        cols = pl.ds(pl.multiple_of(half * nj * kc + j * kc, kc), kc)
        value = jnp.dot(attended, wo[:, cols], preferred_element_type=F32)
        return value.reshape(chips, 8, kc)

    def h_copy(j):
        return remote(theirs.at[j], heard.at[j], h_send.at[j], h_recv.at[j], p.sib)

    def hand(j):
        theirs[j] = product(1 - c, j).astype(BF16)
        h_copy(j).start()

    def e_up(t, j):
        return remote(
            eu.at[t - 1, j], eu.at[t, j], e_send.at[0, j], e_ru.at[t - 1, j], p.up
        )

    def e_dn(t, j):
        return remote(
            ed.at[t - 1, j], ed.at[t, j], e_send.at[1, j], e_rd.at[t - 1, j], p.dn
        )

    def e_own(chip, j):
        return mine[j, chip] + heard[j, chip].astype(F32)

    hand(0)
    for j in range(nj):
        if j + 1 < nj:
            hand(j + 1)
        mine[j] = product(c, j)
        h_copy(j).wait_recv()
        eu[0, j] = e_own(p.chip(ups), j).astype(BF16)
        e_up(1, j).start()
        ed[0, j] = e_own(p.chip(-dns), j).astype(BF16)
        e_dn(1, j).start()

    def e_up_step(t, j):
        e_up(t - 1, j).wait_recv()
        eu[t - 1, j] = (eu[t - 1, j].astype(F32) + e_own(p.chip(ups + 1 - t), j)).astype(BF16)
        e_up(t, j).start()

    def e_dn_step(t, j):
        e_dn(t - 1, j).wait_recv()
        ed[t - 1, j] = (ed[t - 1, j].astype(F32) + e_own(p.chip(t - 1 - dns), j)).astype(BF16)
        e_dn(t, j).start()

    def e_step(t, carry):
        for j in range(nj):
            e_up_step(t, j)
            e_dn_step(t, j)
        return carry

    lax.fori_loop(2, dns + 1, e_step, 0)
    for j in range(nj):
        e_up_step(ups, j)

    first = c == 0

    def t_copy(j):
        return remote(tail.at[j], tail_in.at[j], t_send.at[j], t_recv.at[j], p.sib)

    def put(half, j, value):
        cols = pl.ds(pl.multiple_of(half * nj * kc + j * kc, kc), kc)
        out[:, cols] = (states[:, cols].astype(F32) + value).astype(BF16)

    for j in range(nj):
        e_dn(dns, j).wait_recv()
        e_up(ups, j).wait_recv()
        value = eu[ups, j].astype(F32) + ed[dns, j].astype(F32) + e_own(z, j)
        low, high = value[0:4], value[4:8]
        tail[j] = jnp.where(first, high, low)
        t_copy(j).start()
        put(c, j, jnp.where(first, low, high))
    for j in range(nj):
        t_copy(j).wait_recv()
        put(1 - c, j, tail_in[j])

    wait_bytes(sb, b_send.at[0])
    for j in range(nd):
        part = pl.ds(0, rows)
        wait_bytes(du.at[pl.ds(0, ups), part], d_send.at[0, j])
        wait_bytes(du.at[pl.ds(0, dns), part], d_send.at[1, j])
    for j in range(nj):
        h_copy(j).wait_send()
        wait_bytes(eu.at[pl.ds(0, ups), 0], e_send.at[0, j])
        wait_bytes(eu.at[pl.ds(0, dns), 0], e_send.at[1, j])
        t_copy(j).wait_send()


def project(states, parts, wo, n):
    r, d = states.shape
    nd, nj = 2, 4
    chips = n // 2
    ups, dns = chips // 2, chips - 1 - chips // 2
    rows = 8 * chips
    width = wo.shape[0]
    kc = d // (2 * nj)
    dma = pltpu.SemaphoreType.DMA
    vmem = pltpu.VMEM
    vm = pl.BlockSpec(memory_space=pltpu.VMEM)
    return pl.pallas_call(
        functools.partial(project_kernel, n, nd, nj),
        name="project_out",
        out_shape=jax.ShapeDtypeStruct((r, d), BF16),
        in_specs=[vm, vm, pl.BlockSpec(memory_space=pl.ANY)],
        out_specs=vm,
        scratch_shapes=[
            vmem(wo.shape, BF16),
            vmem((chips, rows, width), BF16),
            vmem((ups + 1, rows, width), BF16),
            vmem((dns + 1, rows, width), BF16),
            vmem((rows, width), BF16),
            vmem((nj, chips, 8, kc), F32),
            vmem((nj, chips, 8, kc), BF16),
            vmem((nj, chips, 8, kc), BF16),
            vmem((ups + 1, nj, 8, kc), BF16),
            vmem((dns + 1, nj, 8, kc), BF16),
            vmem((nj, 4, kc), F32),
            vmem((nj, 4, kc), F32),
            dma((1,)),
            dma((1,)),
            dma((chips,)),
            dma((2, nd)),
            dma((ups, nd)),
            dma((dns, nd)),
            dma((nj,)),
            dma((nj,)),
            dma((2, nj)),
            dma((ups, nj)),
            dma((dns, nj)),
            dma((nj,)),
            dma((nj,)),
        ],
        compiler_params=pltpu.CompilerParams(collective_id=1, has_side_effects=True),
    )(states, parts, wo)


def solution(mesh):
    n = mesh.shape["gx"]

    def local(states, gain, wq, wkv, wo, keys, values, ids, occ):
        qall, kvall = gather(states, gain.reshape(1, -1), wq, wkv, n)
        kvall = kvall.reshape(2, -1, kvall.shape[-1])
        parts = attend(ids, occ, qall, kvall, keys, values)
        return project(states, parts, wo, n)

    both = ("grp", "gx")
    placed = (
        P(both, None),
        P(),
        P(None, "gx"),
        P("gx", None),
        P("gx", None),
        P(both, None, None),
        P(both, None, None),
        P("grp"),
        P(both),
    )
    return jax.shard_map(
        local, mesh=mesh, in_specs=placed, out_specs=P(both, None), check_vma=False
    )
```

time: 489 us -> 178 us (0.36); the launches traced: 480 us -> 178 us
  waiting for transfers between devices: 333 us -> 0 us
  Pallas kernels: 0 us -> 174 us
  blocking collectives: 51.2 us -> 0 us
  local copies, waits for them, and re-layouts: 34.4 us -> 4.42 us
  matrix products: 26.6 us -> 0 us
  between operations: 14 us -> 0.03 us
  starting transfers between devices: 12.6 us -> 0 us
  other arithmetic: 8.13 us -> 0 us
    unnamed x7 -> x0, waiting for transfers between devices: 183 us -> none
    pallas_call x0 -> x3, Pallas kernels: none -> 174 us  [the longest x1 99.5 us: gather(): pl.pallas_call(functools.partial(gather_kernel, n, nj, nq), name='gather_...]
    all_gather x1 -> x0, waiting for transfers between devices: 77.6 us -> none  [local(): lax.all_gather(normalize(remaining_states, scaling_factor_vector), GX, ax...]
    all_to_all x1 -> x0, blocking collectives: 51.2 us -> none  [local(): lax.all_to_all(attended, GX, split_axis=1, concat_axis=0, tiled=True)]
    reduce_scatter x2 -> x0, waiting for transfers between devices: 36.5 us -> none  [sum_in_order(): pieces = lax.psum_scatter(pieces, axes[k], scatter_dimension=0, tiled=True)]
    all_to_all x1 -> x0, waiting for transfers between devices: 36.1 us -> none  [local(): lax.all_to_all(query_slots, GX, split_axis=0, concat_axis=1, tiled=True)]
    dot_general x6 -> x0, matrix products: 26.6 us -> none  [the longest x1 8.2 us: local(): jnp.dot(sliced, final_projection_matrix, preferred_element_type=jnp.float32)]
    all_to_all x1 -> x0, starting transfers between devices: 12.3 us -> none  [local(): lax.all_to_all(query_slots, GX, split_axis=0, concat_axis=1, tiled=True)]
  transfers between devices with their start and end apart: 6 -> 0, of which waited for: 6 -> 0; matrix products, arithmetic and copies ran while one was open for 3% -> 0% of each run, Pallas kernels for 0% -> 0%
where the time goes in v1:
time: 178 us
  Pallas kernels  174 us (98%)
  local copies, waits for them, and re-layouts  4.42 us (2%)
    pallas_call x1, Pallas kernels, gather(): pl.pallas_call(functools.partial(gather_kernel, n, nj, nq), name='gather_...  99.5 us
    pallas_call x1, Pallas kernels, project(): pl.pallas_call(functools.partial(project_kernel, n, nd, nj), name='projec...  64.5 us
    pallas_call x1, Pallas kernels, attend(): pl.pallas_call(attend_kernel, name='attend_slots', out_shape=jax.ShapeDty...  9.63 us

profile of v1, /device:TPU:69, one launch (start us, length us, event | category | flops | bytes accessed | tf_op | source)
XLA Modules:
  0.0 178.0 jit_solution(3414648305781314342)
XLA Ops:
  0.0 1.4 reshape.14.gain
  1.4 1.4 copy.10.ids_col
  2.8 99.5 %gather_queries.1 = (bf16[32,128,256]{2,1,0:T(8,128)(2,1)}, bf16[2,16,8,512]{3,2,1,0:T(8,128)(2,1)}) custom-call(bf16[4,16384]{1,0:T(4,128)(2,1)} %states.3, bf16[1,16384]{1,0:T(2,128)(2,1)} %reshape.14.gain, bf16[16384,256]{1,0:T(8,128)(2,1)} %wq_hbm.1, bf16[512,1024]{1,0:T(8,128)(2,1)} %wkv_hbm.1), custom_call_target="tpu_custom_call" | custom-call | tf_op jit(solution)/shard_map/gather_queries/pallas_call | solution.py:372
  102.3 9.6 %attend_slots.1.parts = bf16[32,128,256]{2,1,0:T(8,128)(2,1)} custom-call(s32[128]{0:T(128)} %ids_s.1, s32[32]{0:T(128)} %occ_s.1, s32[1,128]{1,0:T(1,128)} %bitcast.5, s32[128,1]{1,0:T(8,128)} %copy.10.ids_col, bf16[32,128,256]{2,1,0:T(8,128)(2,1)} %get-tuple-element.7.qall, bf16[2,128,512]{2,1,0:T(8,128)(2,1)} %bitcast.3, bf16[32,128,512]{2,1,0:T(8,128)(2,1)} %k_hbm.1, ...), custom_call_target="tpu_custom_call" | custom-call | tf_op jit(solution)/shard_map/attend_slots/pallas_call | solution.py:535
  111.9 64.5 %project_out.1 = bf16[4,16384]{1,0:T(4,128)(2,1)} custom-call(bf16[4,16384]{1,0:T(4,128)(2,1)} %states.3, bf16[32,128,256]{2,1,0:T(8,128)(2,1)} %attend_slots.1.parts, bf16[256,16384]{1,0:T(8,128)(2,1)} %wo_hbm.1), custom_call_target="tpu_custom_call" | custom-call | tf_op jit(solution)/shard_map/project_out/pallas_call | solution.py:780
  176.4 1.6 copy.12
